TPU v7x, 32 devices: a whole 2x2x4 slice. The times are simulated.
32 devices in a mesh: row: 8 (over y, x, core), col: 4 (over z).
Axes of the slice: x: 2, y: 2, z: 4, core: 2. Of those that a mesh axis runs over, the one named last changes fastest.
Arguments:
- columns: float32 [4096, 8192], P('col', 'row'), may hold values from -64 to 64
- block_order: int32 [64], P('col'), may hold values from 0 to 63, as said below
Outputs:
- rotated: float32 [4096, 8192], P('col', 'row')
Inputs may be any that keep to these rules, and one draw needn't show every extreme that they name: block_order is a permutation of 0 .. 63 in which slots c * 16 to (c + 1) * 16 - 1 name blocks c * 16 to (c + 1) * 16 - 1.
All inputs are finite; a program needn't handle non-finite values.
Results may differ from a plain program's by a relative error of at most 0.00055.
Values sent between devices are 32-bit elements; how exact they have to be, the bound alone decides.
No kernel may reach another device: no remote copies, remote signals or barrier semaphores. Data moves between devices by JAX's collectives and lax.ppermute only.
A program may use at most 64 MiB of HBM per device.

v0:
```python
import jax
import jax.numpy as jnp
from jax import lax
from jax.sharding import PartitionSpec as P

BLOCK = 64
STEPS = 4


def shifted(value, axis, steps):
    count = lax.axis_size(axis)
    leading, last = (max(0, -steps), min(count, count - steps))
    return lax.ppermute(value, axis, [(source, source + steps) for source in range(leading, last)])


def make_systems(cross_sum, col_norms):
    highest = lax.Precision.HIGHEST
    top_norms = col_norms[:, :BLOCK][:, :, None]
    bottom_norms = col_norms[:, BLOCK:][:, None, :]
    spread = bottom_norms - top_norms
    radius = jnp.sqrt(spread * spread + 4.0 * cross_sum * cross_sum)
    scale_term = (top_norms + bottom_norms) / BLOCK
    coupling = (
        2.0
        * cross_sum
        * spread
        / (
            spread * spread
            + 4.0 * cross_sum * cross_sum
            + jnp.abs(spread) * radius
            + scale_term * scale_term
        )
    )
    identity = jnp.eye(BLOCK, dtype=jnp.float32)
    left_system = identity + jnp.einsum("pij,pkj->pik", coupling, coupling, precision=highest)
    right_system = identity + jnp.einsum("pji,pjk->pik", coupling, coupling, precision=highest)
    identities = jnp.broadcast_to(identity, coupling.shape)
    upper_half = jnp.concatenate([identities, coupling], axis=2)
    lower_half = jnp.concatenate([-jnp.transpose(coupling, (0, 2, 1)), identities], axis=2)
    systems = jnp.concatenate([left_system, right_system], axis=0)
    targets = jnp.concatenate([upper_half, lower_half], axis=0)
    return (systems, targets)


def solve_systems(systems, targets):
    factors = jnp.linalg.cholesky(systems)

    def solve_one(factor, target):
        return jax.scipy.linalg.cho_solve((factor, True), target)

    return jax.vmap(solve_one)(factors, targets)


def finish_turn(targets, solved_all):
    highest = lax.Precision.HIGHEST
    pairs = targets.shape[0] // 2
    solved = jnp.concatenate([solved_all[:pairs], solved_all[pairs:]], axis=1)
    plus_skew = jnp.concatenate([targets[:pairs], targets[pairs:]], axis=1)
    return jnp.einsum("pij,pjk->pik", plus_skew, solved, precision=highest)


def cayley_turn(cross_sum, col_norms):
    systems, targets = make_systems(cross_sum, col_norms)
    total = systems.shape[0]
    groups = lax.axis_size("row")
    share = -(-total // groups)
    start = lax.axis_index("row") * share
    mine_systems = lax.dynamic_slice_in_dim(systems, start, share, 0)
    mine_targets = lax.dynamic_slice_in_dim(targets, start, share, 0)
    mine_solved = solve_systems(mine_systems, mine_targets)
    gathered = lax.all_gather(mine_solved, "row", axis=0, tiled=True)
    return finish_turn(targets, gathered)


def local(columns, block_order):
    highest = lax.Precision.HIGHEST
    width, length = columns.shape
    count = width // BLOCK
    position = lax.axis_index("col")
    last_index = lax.axis_size("col") - 1
    local_index = block_order - position * block_order.shape[0]
    blocks = jnp.take(columns.reshape(count, BLOCK, length), local_index, axis=0)
    blocks = blocks.reshape(count // 2, 2 * BLOCK, length)
    for sweep_step in range(STEPS):
        cross_part = jnp.einsum(
            "pim,pjm->pij", blocks[:, :BLOCK], blocks[:, BLOCK:], precision=highest
        )
        norm_part = jnp.sum(blocks * blocks, axis=2)
        cross_sum, col_norms = lax.psum((cross_part, norm_part), "row")
        turn_matrix = cayley_turn(cross_sum, col_norms)
        turned = jnp.einsum("pij,pim->pjm", turn_matrix, blocks, precision=highest)
        top_blocks = turned[:, :BLOCK]
        bottom_blocks = turned[:, BLOCK:]
        from_left = shifted(top_blocks[-1], "col", 1)
        from_right = shifted(bottom_blocks[0], "col", -1)
        first_top = jnp.where(position == 0, top_blocks[0], from_left)
        second_top = jnp.where(position == 0, bottom_blocks[0], top_blocks[0])
        new_tops = jnp.concatenate([first_top[None], second_top[None], top_blocks[1:-1]], axis=0)
        last_bottom = jnp.where(position == last_index, top_blocks[-1], from_right)
        new_bottoms = jnp.concatenate([bottom_blocks[1:], last_bottom[None]], axis=0)
        blocks = jnp.concatenate([new_tops, new_bottoms], axis=1)
    return blocks.reshape(width, length)


def solution(mesh):
    placed = (P("col", "row"), P("col"))
    return jax.shard_map(
        local, mesh=mesh, in_specs=placed, out_specs=P("col", "row"), check_vma=False
    )
```

profile of v0, /device:TPU:0, one launch (start us, length us, event | category | flops | bytes accessed | tf_op | source)
XLA Modules:
  0.0 517.0 jit_solution(15705440596389083100)
XLA Ops:
  7.5 5.0 gather_fusion
  12.5 2.5 bitcast_select_fusion
  15.0 1.9 copy-done
  17.0 2.9 fusion
  19.9 2.7 multiply_reduce_fusion.3
  22.7 15.1 %psum.57 = f32[8,128]{1,0:T(8,128)S(1)} all-reduce(f32[8,128]{1,0:T(8,128)S(1)} %reduce_sum.39), channel_id=1, replica_groups=mesh['row'=8,'col'=4] {'row'}, use_global_device_ids=true, to_apply=%region_2.3 | all-reduce | flops 1024 | bytes 8192 | tf_op jit(solution)/shard_map/psum | solution.py:89
  38.1 38.6 %all-reduce.5.cloned.1.call-done = f32[8,64,64]{1,2,0:T(8,128)} async-done(((f32[8,64,64]{1,2,0:T(8,128)}), f32[8,64,64]{1,2,0:T(8,128)}) %all-reduce.5.cloned.1.call-update) | async-done | bytes 131088 | tf_op jit(solution)/shard_map/psum | solution.py:89
  79.3 11.7 %custom-call.14 = f32[2,64,64]{2,1,0:T(8,128)S(1)} custom-call(f32[2,64,64]{2,1,0:T(8,128)S(1)} %fusion.135), custom_call_target="Cholesky" | custom-call | tf_op jit(solution)/shard_map/jit(cholesky)/cholesky | solution.py:46
  91.2 9.8 %custom-call.15 = f32[2,1,64,64]{2,3,1,0:T(8,128)S(1)} custom-call(f32[2,1,64,64]{3,2,1,0:T(8,128)S(1)} %select_bitcast_fusion.7), custom_call_target="InvertDiagBlocksLowerTriangular" | custom-call | tf_op jit(solution)/shard_map/vmap(jit(_cho_solve))/triangular_solve | solution.py:49
  101.7 9.8 %all_gather.12 = f32[16,64,128]{2,1,0:T(8,128)S(1)} all-gather(f32[2,64,128]{2,1,0:T(8,128)S(1)} %fusion.132), channel_id=1, replica_groups=mesh['row'=8,'col'=4] {'row'}, dimensions={0}, use_global_device_ids=true | all-gather | bytes 589824 | tf_op jit(solution)/shard_map/all_gather | solution.py:71
  112.8 4.1 fusion.167
  116.9 2.0 copy-done.2
  119.0 3.4 collective-permute-start
  123.7 1.6 slice.214
  125.4 1.5 slice.213
  126.9 1.6 collective-permute-done
  128.5 4.1 collective-permute-done.1
  134.5 2.9 fusion.3
  137.4 12.1 %psum.59 = f32[8,128]{1,0:T(8,128)S(1)} all-reduce(f32[8,128]{1,0:T(8,128)S(1)} %multiply_reduce_fusion.2), channel_id=1, replica_groups=mesh['row'=8,'col'=4] {'row'}, use_global_device_ids=true, to_apply=%region_7.10 | all-reduce | flops 1024 | bytes 8192 | tf_op jit(solution)/shard_map/psum | solution.py:89
  149.8 52.5 %all-reduce.7.cloned.1.call-done = f32[8,64,64]{1,2,0:T(8,128)} async-done(((f32[8,64,64]{1,2,0:T(8,128)}), f32[8,64,64]{1,2,0:T(8,128)}) %all-reduce.7.cloned.1.call-update) | async-done | bytes 131088 | tf_op jit(solution)/shard_map/psum | solution.py:89
  207.1 12.5 %custom-call.16 = f32[2,64,64]{2,1,0:T(8,128)S(1)} custom-call(f32[2,64,64]{2,1,0:T(8,128)} %fusion.131), custom_call_target="Cholesky" | custom-call | tf_op jit(solution)/shard_map/jit(cholesky)/cholesky | solution.py:46
  220.4 10.6 %custom-call.17 = f32[2,1,64,64]{2,3,1,0:T(8,128)S(1)} custom-call(f32[2,1,64,64]{3,2,1,0:T(8,128)} %select_bitcast_fusion.6), custom_call_target="InvertDiagBlocksLowerTriangular" | custom-call | tf_op jit(solution)/shard_map/vmap(jit(_cho_solve))/triangular_solve | solution.py:49
  231.6 9.2 %all_gather.13 = f32[16,64,128]{2,1,0:T(8,128)S(1)} all-gather(f32[2,64,128]{2,1,0:T(8,128)S(1)} %fusion.128), channel_id=1, replica_groups=mesh['row'=8,'col'=4] {'row'}, dimensions={0}, use_global_device_ids=true | all-gather | bytes 589824 | tf_op jit(solution)/shard_map/all_gather | solution.py:71
  242.1 3.8 fusion.32
  246.0 3.4 collective-permute-start.2
  251.2 4.2 collective-permute-done.2
  255.4 4.1 collective-permute-done.3
  260.4 2.9 fusion.12
  263.3 12.0 %psum.61 = f32[8,128]{1,0:T(8,128)S(1)} all-reduce(f32[8,128]{1,0:T(8,128)S(1)} %multiply_reduce_fusion.1), channel_id=1, replica_groups=mesh['row'=8,'col'=4] {'row'}, use_global_device_ids=true, to_apply=%region_10.13 | all-reduce | flops 1024 | bytes 8192 | tf_op jit(solution)/shard_map/psum | solution.py:89
  275.5 52.7 %all-reduce.9.cloned.1.call-done = f32[8,64,64]{1,2,0:T(8,128)} async-done(((f32[8,64,64]{1,2,0:T(8,128)}), f32[8,64,64]{1,2,0:T(8,128)}) %all-reduce.9.cloned.1.call-update) | async-done | bytes 131088 | tf_op jit(solution)/shard_map/psum | solution.py:89
  333.0 12.5 %custom-call.18 = f32[2,64,64]{2,1,0:T(8,128)S(1)} custom-call(f32[2,64,64]{2,1,0:T(8,128)} %fusion.127), custom_call_target="Cholesky" | custom-call | tf_op jit(solution)/shard_map/jit(cholesky)/cholesky | solution.py:46
  346.4 10.6 %custom-call.19 = f32[2,1,64,64]{2,3,1,0:T(8,128)S(1)} custom-call(f32[2,1,64,64]{3,2,1,0:T(8,128)} %select_bitcast_fusion.5), custom_call_target="InvertDiagBlocksLowerTriangular" | custom-call | tf_op jit(solution)/shard_map/vmap(jit(_cho_solve))/triangular_solve | solution.py:49
  357.5 9.4 %all_gather.14 = f32[16,64,128]{2,1,0:T(8,128)S(1)} all-gather(f32[2,64,128]{2,1,0:T(8,128)S(1)} %fusion.124), channel_id=1, replica_groups=mesh['row'=8,'col'=4] {'row'}, dimensions={0}, use_global_device_ids=true | all-gather | bytes 589824 | tf_op jit(solution)/shard_map/all_gather | solution.py:71
  368.2 3.8 fusion.31
  372.1 3.4 collective-permute-start.4
  377.2 4.4 collective-permute-done.4
  381.6 4.1 collective-permute-done.5
  386.3 2.9 fusion.21
  389.2 12.3 %psum.63 = f32[8,128]{1,0:T(8,128)S(1)} all-reduce(f32[8,128]{1,0:T(8,128)S(1)} %multiply_reduce_fusion), channel_id=1, replica_groups=mesh['row'=8,'col'=4] {'row'}, use_global_device_ids=true, to_apply=%region_13.16 | all-reduce | flops 1024 | bytes 8192 | tf_op jit(solution)/shard_map/psum | solution.py:89
  401.6 52.8 %all-reduce.11.cloned.1.call-done = f32[8,64,64]{1,2,0:T(8,128)} async-done(((f32[8,64,64]{1,2,0:T(8,128)}), f32[8,64,64]{1,2,0:T(8,128)}) %all-reduce.11.cloned.1.call-update) | async-done | bytes 131088 | tf_op jit(solution)/shard_map/psum | solution.py:89
  456.9 11.7 %custom-call.20 = f32[2,64,64]{2,1,0:T(8,128)S(1)} custom-call(f32[2,64,64]{2,1,0:T(8,128)S(1)} %fusion.123), custom_call_target="Cholesky" | custom-call | tf_op jit(solution)/shard_map/jit(cholesky)/cholesky | solution.py:46
  468.9 9.8 %custom-call.21 = f32[2,1,64,64]{2,3,1,0:T(8,128)S(1)} custom-call(f32[2,1,64,64]{3,2,1,0:T(8,128)S(1)} %select_bitcast_fusion.4), custom_call_target="InvertDiagBlocksLowerTriangular" | custom-call | tf_op jit(solution)/shard_map/vmap(jit(_cho_solve))/triangular_solve | solution.py:49
  479.5 9.2 %all_gather.15 = f32[16,64,128]{2,1,0:T(8,128)S(1)} all-gather(f32[2,64,128]{2,1,0:T(8,128)S(1)} %fusion.120), channel_id=1, replica_groups=mesh['row'=8,'col'=4] {'row'}, dimensions={0}, use_global_device_ids=true | all-gather | bytes 589824 | tf_op jit(solution)/shard_map/all_gather | solution.py:71
  489.9 3.8 fusion.30
  493.8 3.4 collective-permute-start.6
  498.7 4.5 collective-permute-done.6
  503.3 4.1 collective-permute-done.7
  507.4 2.5 maximum_maximum_fusion.3
  (141 shorter events, 35.6 us)
Async XLA Ops:
  6.5 70.1 %all-reduce.5.cloned.1.call-start = ((), (), s32[]{:S(2)}) async-start(), calls=%async_computation | async-start | bytes 524288 | tf_op jit(solution)/shard_map/psum | solution.py:89
  15.0 1.9 copy-start
  19.8 182.5 %all-reduce.7.cloned.1.call-start = ((), (), s32[]{:S(2)}) async-start(), calls=%async_computation.1 | async-start | bytes 524288 | tf_op jit(solution)/shard_map/psum | solution.py:89
  101.1 11.7 %copy-start.1 = (f32[8,128,1024]{2,1,0:T(8,128)S(1)}, f32[8,128,1024]{2,1,0:T(8,128)}, u32[]{:S(2)}) copy-start(f32[8,128,1024]{2,1,0:T(8,128)} %copy-done) | copy-start | bytes 12582916
  116.9 2.0 copy-start.2
  119.0 15.2 %copy-start.9 = (f32[1,64,1024]{2,1,0:T(8,128)}, f32[1,64,1024]{2,1,0:T(8,128)S(1)}, u32[]{:S(2)}) copy-start(f32[1,64,1024]{2,1,0:T(8,128)S(1)} %get-tuple-element.35) | copy-start | bytes 786436
  119.0 9.5 %collective-permute-start = (f32[64,1024]{1,0:T(8,128)S(1)}, f32[64,1024]{1,0:T(8,128)S(1)}, u32[]{:S(2)}, u32[]{:S(2)}) collective-permute-start(f32[64,1024]{1,0:T(8,128)S(1)} %get-tuple-element.36), channel_id=1, source_target_pairs={{0,1},{1,2},{2,3},{4,5},{5,6},{6,7},{8,9},{9,10},{10,11},{12,13},{... | collective-permute-start | bytes 786440 | tf_op jit(solution)/shard_map/ppermute | solution.py:13
  122.4 10.2 %collective-permute-start.1 = (f32[64,1024]{1,0:T(8,128)S(1)}, f32[64,1024]{1,0:T(8,128)S(1)}, u32[]{:S(2)}, u32[]{:S(2)}) collective-permute-start(f32[64,1024]{1,0:T(8,128)S(1)} %get-tuple-element.34), channel_id=1, source_target_pairs={{1,0},{2,1},{3,2},{5,4},{6,5},{7,6},{9,8},{10,9},{11,10},{13,12},{... | collective-permute-start | bytes 786440 | tf_op jit(solution)/shard_map/ppermute | solution.py:13
  126.9 7.3 %copy-start.7 = (f32[6,64,1024]{2,1,0:T(8,128)}, f32[6,64,1024]{2,1,0:T(8,128)S(1)}, u32[]{:S(2)}) copy-start(f32[6,64,1024]{2,1,0:T(8,128)S(1)} %slice.213) | copy-start | bytes 4718596
  133.7 0.7 copy-start.17
  133.7 0.8 copy-start.19
  149.5 178.7 %all-reduce.9.cloned.1.call-start = ((), (), s32[]{:S(2)}) async-start(), calls=%async_computation.2 | async-start | bytes 524288 | tf_op jit(solution)/shard_map/psum | solution.py:89
  204.9 37.2 %copy-start.10 = (f32[1,64,1024]{2,1,0:T(8,128)S(1)}, f32[1,64,1024]{2,1,0:T(8,128)}, u32[]{:S(2)}) copy-start(f32[1,64,1024]{2,1,0:T(8,128)} %copy-done.9) | copy-start | bytes 786436
  204.9 37.1 %copy-start.18 = (f32[1,64,1024]{2,1,0:T(8,128)S(1)}, f32[1,64,1024]{2,1,0:T(8,128)}, u32[]{:S(2)}) copy-start(f32[1,64,1024]{2,1,0:T(8,128)} %copy-done.17) | copy-start | bytes 786436
  204.9 37.1 %copy-start.20 = (f32[1,64,1024]{2,1,0:T(8,128)S(1)}, f32[1,64,1024]{2,1,0:T(8,128)}, u32[]{:S(2)}) copy-start(f32[1,64,1024]{2,1,0:T(8,128)} %copy-done.19) | copy-start | bytes 786436
  231.0 11.0 %copy-start.8 = (f32[6,64,1024]{2,1,0:T(8,128)S(1)}, f32[6,64,1024]{2,1,0:T(8,128)}, u32[]{:S(2)}) copy-start(f32[6,64,1024]{2,1,0:T(8,128)} %copy-done.7) | copy-start | bytes 4718596
  246.0 14.2 %copy-start.11 = (f32[1,64,1024]{2,1,0:T(8,128)}, f32[1,64,1024]{2,1,0:T(8,128)S(1)}, u32[]{:S(2)}) copy-start(f32[1,64,1024]{2,1,0:T(8,128)S(1)} %get-tuple-element.30) | copy-start | bytes 786436
  246.0 9.5 %collective-permute-start.2 = (f32[64,1024]{1,0:T(8,128)S(1)}, f32[64,1024]{1,0:T(8,128)S(1)}, u32[]{:S(2)}, u32[]{:S(2)}) collective-permute-start(f32[64,1024]{1,0:T(8,128)S(1)} %get-tuple-element.31), channel_id=1, source_target_pairs={{0,1},{1,2},{2,3},{4,5},{5,6},{6,7},{8,9},{9,10},{10,11},{12,13},{... | collective-permute-start | bytes 786440 | tf_op jit(solution)/shard_map/ppermute | solution.py:13
  249.4 10.2 %collective-permute-start.3 = (f32[64,1024]{1,0:T(8,128)S(1)}, f32[64,1024]{1,0:T(8,128)S(1)}, u32[]{:S(2)}, u32[]{:S(2)}) collective-permute-start(f32[64,1024]{1,0:T(8,128)S(1)} %get-tuple-element.29), channel_id=1, source_target_pairs={{1,0},{2,1},{3,2},{5,4},{6,5},{7,6},{9,8},{10,9},{11,10},{13,12},{... | collective-permute-start | bytes 786440 | tf_op jit(solution)/shard_map/ppermute | solution.py:13
  251.2 8.9 %copy-start.5 = (f32[6,64,1024]{2,1,0:T(8,128)}, f32[6,64,1024]{2,1,0:T(8,128)S(1)}, u32[]{:S(2)}) copy-start(f32[6,64,1024]{2,1,0:T(8,128)S(1)} %slice.220) | copy-start | bytes 4718596
  259.6 0.7 copy-start.13
  259.6 0.8 copy-start.15
  275.4 179.0 %all-reduce.11.cloned.1.call-start = ((), (), s32[]{:S(2)}) async-start(), calls=%async_computation.3 | async-start | bytes 524288 | tf_op jit(solution)/shard_map/psum | solution.py:89
  330.8 37.4 %copy-start.12 = (f32[1,64,1024]{2,1,0:T(8,128)S(1)}, f32[1,64,1024]{2,1,0:T(8,128)}, u32[]{:S(2)}) copy-start(f32[1,64,1024]{2,1,0:T(8,128)} %copy-done.11) | copy-start | bytes 786436
  330.8 37.4 %copy-start.14 = (f32[1,64,1024]{2,1,0:T(8,128)S(1)}, f32[1,64,1024]{2,1,0:T(8,128)}, u32[]{:S(2)}) copy-start(f32[1,64,1024]{2,1,0:T(8,128)} %copy-done.13) | copy-start | bytes 786436
  330.8 37.4 %copy-start.16 = (f32[1,64,1024]{2,1,0:T(8,128)S(1)}, f32[1,64,1024]{2,1,0:T(8,128)}, u32[]{:S(2)}) copy-start(f32[1,64,1024]{2,1,0:T(8,128)} %copy-done.15) | copy-start | bytes 786436
  356.9 11.3 %copy-start.6 = (f32[6,64,1024]{2,1,0:T(8,128)S(1)}, f32[6,64,1024]{2,1,0:T(8,128)}, u32[]{:S(2)}) copy-start(f32[6,64,1024]{2,1,0:T(8,128)} %copy-done.5) | copy-start | bytes 4718596
  372.1 9.5 %collective-permute-start.4 = (f32[64,1024]{1,0:T(8,128)S(1)}, f32[64,1024]{1,0:T(8,128)S(1)}, u32[]{:S(2)}, u32[]{:S(2)}) collective-permute-start(f32[64,1024]{1,0:T(8,128)S(1)} %get-tuple-element.26), channel_id=1, source_target_pairs={{0,1},{1,2},{2,3},{4,5},{5,6},{6,7},{8,9},{9,10},{10,11},{12,13},{... | collective-permute-start | bytes 786440 | tf_op jit(solution)/shard_map/ppermute | solution.py:13
  375.5 10.2 %collective-permute-start.5 = (f32[64,1024]{1,0:T(8,128)S(1)}, f32[64,1024]{1,0:T(8,128)S(1)}, u32[]{:S(2)}, u32[]{:S(2)}) collective-permute-start(f32[64,1024]{1,0:T(8,128)S(1)} %get-tuple-element.24), channel_id=1, source_target_pairs={{1,0},{2,1},{3,2},{5,4},{6,5},{7,6},{9,8},{10,9},{11,10},{13,12},{... | collective-permute-start | bytes 786440 | tf_op jit(solution)/shard_map/ppermute | solution.py:13
  377.2 9.1 %copy-start.3 = (f32[6,64,1024]{2,1,0:T(8,128)}, f32[6,64,1024]{2,1,0:T(8,128)S(1)}, u32[]{:S(2)}) copy-start(f32[6,64,1024]{2,1,0:T(8,128)S(1)} %slice.227) | copy-start | bytes 4718596
  478.8 11.1 %copy-start.4 = (f32[6,64,1024]{2,1,0:T(8,128)S(1)}, f32[6,64,1024]{2,1,0:T(8,128)}, u32[]{:S(2)}) copy-start(f32[6,64,1024]{2,1,0:T(8,128)} %copy-done.3) | copy-start | bytes 4718596
  493.8 9.5 %collective-permute-start.6 = (f32[64,1024]{1,0:T(8,128)S(1)}, f32[64,1024]{1,0:T(8,128)S(1)}, u32[]{:S(2)}, u32[]{:S(2)}) collective-permute-start(f32[64,1024]{1,0:T(8,128)S(1)} %get-tuple-element.19), channel_id=1, source_target_pairs={{0,1},{1,2},{2,3},{4,5},{5,6},{6,7},{8,9},{9,10},{10,11},{12,13},{... | collective-permute-start | bytes 786440 | tf_op jit(solution)/shard_map/ppermute | solution.py:13
  497.2 10.2 %collective-permute-start.7 = (f32[64,1024]{1,0:T(8,128)S(1)}, f32[64,1024]{1,0:T(8,128)S(1)}, u32[]{:S(2)}, u32[]{:S(2)}) collective-permute-start(f32[64,1024]{1,0:T(8,128)S(1)} %get-tuple-element.20), channel_id=1, source_target_pairs={{1,0},{2,1},{3,2},{5,4},{6,5},{7,6},{9,8},{10,9},{11,10},{13,12},{... | collective-permute-start | bytes 786440 | tf_op jit(solution)/shard_map/ppermute | solution.py:13
Sparse Core Ops, SparseCore 0:
  20.0 56.6 all-reduce.4
  149.6 52.6 all-reduce.6
  275.5 52.6 all-reduce.8
  401.6 52.6 all-reduce.10
where the time goes:
time: 524 us; the launch traced here: 517 us
  waiting for transfers between devices  228 us (44%)
  other arithmetic  111 us (21%)
  blocking collectives  89.2 us (17%)
  matrix products  38.7 us (7%)
  starting transfers between devices  19.3 us (4%)
  local copies, waits for them, and re-layouts  16.6 us (3%)
  between operations  14.5 us (3%)
    psum x4, waiting for transfers between devices, local(): cross_sum, col_norms = lax.psum((cross_part, norm_part), 'row')  197 us
    psum x4, blocking collectives, local(): cross_sum, col_norms = lax.psum((cross_part, norm_part), 'row')  51.6 us
    another operation x13, other arithmetic, solve_systems(): factors = jnp.linalg.cholesky(systems)  49 us
    another operation x9, other arithmetic, solve_one(): return jax.scipy.linalg.cho_solve((factor, True), target)  42.4 us
    all_gather x4, blocking collectives, cayley_turn(): gathered = lax.all_gather(mine_solved, 'row', axis=0, tiled=True)  37.7 us
    ppermute x8, waiting for transfers between devices, shifted(): lax.ppermute(value, axis, [(source, source + steps) for source in range(l...  31.2 us
    ppermute x8, starting transfers between devices, shifted(): lax.ppermute(value, axis, [(source, source + steps) for source in range(l...  19 us
    dot_general x4, matrix products, local(): turned = jnp.einsum('pij,pim->pjm', turn_matrix, blocks, precision=highest)  15.6 us
  transfers between devices with their start and end apart: 12, of which 12 were waited for; matrix products, arithmetic and copies ran while one was open for 1% of the time, Pallas kernels for 0%

commit v1 on v0

--- a/solution.py
+++ b/solution.py
@@ -68,7 +68,16 @@
     mine_systems = lax.dynamic_slice_in_dim(systems, start, share, 0)
     mine_targets = lax.dynamic_slice_in_dim(targets, start, share, 0)
     mine_solved = solve_systems(mine_systems, mine_targets)
-    gathered = lax.all_gather(mine_solved, "row", axis=0, tiled=True)
+    size_here = lax.axis_size("row")
+    left_arr = sorted(((b, (b + 1) % size_here) for b in range(size_here)))
+    view_out = mine_solved
+    stack_in = [view_out]
+    for dd in range(1, size_here):
+        view_out = lax.ppermute(view_out, "row", left_arr)
+        stack_in.insert(0, view_out)
+    gathered = jnp.roll(
+        jnp.concatenate(stack_in, 0), (lax.axis_index("row") + 1) * mine_solved.shape[0], 0
+    )
     return finish_turn(targets, gathered)
 
 

time: 524 us -> 606 us (1.16)
  waiting for transfers between devices: 228 us -> 347 us
  blocking collectives: 89.2 us -> 50.5 us
    ppermute x0 -> x28, waiting for transfers between devices: none -> 128 us  [cayley_turn(): view_out = lax.ppermute(view_out, 'row', left_arr)]
    all_gather x4 -> x0, blocking collectives: 37.7 us -> none  [cayley_turn(): gathered = lax.all_gather(mine_solved, 'row', axis=0, tiled=True)]
    ppermute x8, waiting for transfers between devices: 31.2 us -> 23.5 us  [shifted(): lax.ppermute(value, axis, [(source, source + steps) for source in range(l...]
  transfers between devices with their start and end apart: 12 -> 40, of which waited for: 12 -> 39; matrix products, arithmetic and copies ran while one was open for 1% -> 1% of each run, Pallas kernels for 0% -> 0%
where the time goes in v1:
time: 606 us; the launch traced here: 599 us
  waiting for transfers between devices  347 us (57%)
  other arithmetic  111 us (18%)
  blocking collectives  50.5 us (8%)
  matrix products  38.7 us (6%)
  starting transfers between devices  20.3 us (3%)
  local copies, waits for them, and re-layouts  16.9 us (3%)
  between operations  14.6 us (2%)
    psum x4, waiting for transfers between devices, local(): cross_sum, col_norms = lax.psum((cross_part, norm_part), 'row')  195 us
    ppermute x28, waiting for transfers between devices, cayley_turn(): view_out = lax.ppermute(view_out, 'row', left_arr)  128 us
    psum x4, blocking collectives, local(): cross_sum, col_norms = lax.psum((cross_part, norm_part), 'row')  50.5 us
    another operation x13, other arithmetic, solve_systems(): factors = jnp.linalg.cholesky(systems)  49 us
    another operation x9, other arithmetic, solve_one(): return jax.scipy.linalg.cho_solve((factor, True), target)  42.4 us
    ppermute x8, waiting for transfers between devices, shifted(): lax.ppermute(value, axis, [(source, source + steps) for source in range(l...  23.5 us
    ppermute x8, starting transfers between devices, shifted(): lax.ppermute(value, axis, [(source, source + steps) for source in range(l...  19 us
    dot_general x4, matrix products, local(): turned = jnp.einsum('pij,pim->pjm', turn_matrix, blocks, precision=highest)  15.6 us
  transfers between devices with their start and end apart: 40, of which 39 were waited for; matrix products, arithmetic and copies ran while one was open for 1% of the time, Pallas kernels for 0%

profile of v1, /device:TPU:0, one launch (start us, length us, event | category | flops | bytes accessed | tf_op | source)
XLA Modules:
  0.0 599.3 jit_solution(12522642322759520676)
XLA Ops:
  7.5 5.0 gather_fusion
  22.8 15.2 %psum.57 = f32[8,128]{1,0:T(8,128)S(1)} all-reduce(f32[8,128]{1,0:T(8,128)S(1)} %reduce_sum.39), channel_id=1, replica_groups=mesh['row'=8,'col'=4] {'row'}, use_global_device_ids=true, to_apply=%region_2.3 | all-reduce | flops 1024 | bytes 8192 | tf_op jit(solution)/shard_map/psum | solution.py:98
  38.1 38.6 %all-reduce.5.cloned.1.call-done = f32[8,64,64]{1,2,0:T(8,128)} async-done(((f32[8,64,64]{1,2,0:T(8,128)}), f32[8,64,64]{1,2,0:T(8,128)}) %all-reduce.5.cloned.1.call-update) | async-done | bytes 131088 | tf_op jit(solution)/shard_map/psum | solution.py:98
  79.3 11.7 %custom-call.14 = f32[2,64,64]{2,1,0:T(8,128)S(1)} custom-call(f32[2,64,64]{2,1,0:T(8,128)S(1)} %fusion.139), custom_call_target="Cholesky" | custom-call | tf_op jit(solution)/shard_map/jit(cholesky)/cholesky | solution.py:46
  91.3 9.8 %custom-call.15 = f32[2,1,64,64]{2,3,1,0:T(8,128)S(1)} custom-call(f32[2,1,64,64]{3,2,1,0:T(8,128)S(1)} %select_bitcast_fusion.7), custom_call_target="InvertDiagBlocksLowerTriangular" | custom-call | tf_op jit(solution)/shard_map/vmap(jit(_cho_solve))/triangular_solve | solution.py:49
  101.8 4.6 collective-permute-done
  106.4 4.6 collective-permute-done.1
  110.9 4.6 collective-permute-done.2
  115.5 4.6 collective-permute-done.3
  120.1 4.6 collective-permute-done.4
  124.7 4.6 collective-permute-done.5
  129.5 4.5 collective-permute-done.6
  158.3 11.8 %psum.59 = f32[8,128]{1,0:T(8,128)S(1)} all-reduce(f32[8,128]{1,0:T(8,128)S(1)} %multiply_reduce_fusion.2), channel_id=1, replica_groups=mesh['row'=8,'col'=4] {'row'}, use_global_device_ids=true, to_apply=%region_7.11 | all-reduce | flops 1024 | bytes 8192 | tf_op jit(solution)/shard_map/psum | solution.py:98
  170.2 52.4 %all-reduce.7.cloned.1.call-done = f32[8,64,64]{1,2,0:T(8,128)} async-done(((f32[8,64,64]{1,2,0:T(8,128)}), f32[8,64,64]{1,2,0:T(8,128)}) %all-reduce.7.cloned.1.call-update) | async-done | bytes 131088 | tf_op jit(solution)/shard_map/psum | solution.py:98
  227.3 12.5 %custom-call.16 = f32[2,64,64]{2,1,0:T(8,128)S(1)} custom-call(f32[2,64,64]{2,1,0:T(8,128)} %fusion.135), custom_call_target="Cholesky" | custom-call | tf_op jit(solution)/shard_map/jit(cholesky)/cholesky | solution.py:46
  240.6 10.6 %custom-call.17 = f32[2,1,64,64]{2,3,1,0:T(8,128)S(1)} custom-call(f32[2,1,64,64]{3,2,1,0:T(8,128)} %select_bitcast_fusion.6), custom_call_target="InvertDiagBlocksLowerTriangular" | custom-call | tf_op jit(solution)/shard_map/vmap(jit(_cho_solve))/triangular_solve | solution.py:49
  252.1 4.6 collective-permute-done.9
  256.6 4.6 collective-permute-done.10
  261.2 4.6 collective-permute-done.11
  265.8 4.6 collective-permute-done.12
  270.4 4.6 collective-permute-done.13
  275.0 4.6 collective-permute-done.14
  279.6 4.6 collective-permute-done.15
  296.9 4.4 collective-permute-done.17
  305.1 11.8 %psum.61 = f32[8,128]{1,0:T(8,128)S(1)} all-reduce(f32[8,128]{1,0:T(8,128)S(1)} %multiply_reduce_fusion.1), channel_id=1, replica_groups=mesh['row'=8,'col'=4] {'row'}, use_global_device_ids=true, to_apply=%region_10.14 | all-reduce | flops 1024 | bytes 8192 | tf_op jit(solution)/shard_map/psum | solution.py:98
  317.4 51.9 %all-reduce.9.cloned.1.call-done = f32[8,64,64]{1,2,0:T(8,128)} async-done(((f32[8,64,64]{1,2,0:T(8,128)}), f32[8,64,64]{1,2,0:T(8,128)}) %all-reduce.9.cloned.1.call-update) | async-done | bytes 131088 | tf_op jit(solution)/shard_map/psum | solution.py:98
  374.1 12.5 %custom-call.18 = f32[2,64,64]{2,1,0:T(8,128)S(1)} custom-call(f32[2,64,64]{2,1,0:T(8,128)} %fusion.131), custom_call_target="Cholesky" | custom-call | tf_op jit(solution)/shard_map/jit(cholesky)/cholesky | solution.py:46
  387.4 10.6 %custom-call.19 = f32[2,1,64,64]{2,3,1,0:T(8,128)S(1)} custom-call(f32[2,1,64,64]{3,2,1,0:T(8,128)} %select_bitcast_fusion.5), custom_call_target="InvertDiagBlocksLowerTriangular" | custom-call | tf_op jit(solution)/shard_map/vmap(jit(_cho_solve))/triangular_solve | solution.py:49
  398.6 4.6 collective-permute-done.18
  403.2 4.6 collective-permute-done.19
  407.8 4.6 collective-permute-done.20
  412.4 4.6 collective-permute-done.21
  417.0 4.6 collective-permute-done.22
  421.6 4.6 collective-permute-done.23
  426.2 4.6 collective-permute-done.24
  443.4 4.4 collective-permute-done.26
  451.3 11.8 %psum.63 = f32[8,128]{1,0:T(8,128)S(1)} all-reduce(f32[8,128]{1,0:T(8,128)S(1)} %multiply_reduce_fusion), channel_id=1, replica_groups=mesh['row'=8,'col'=4] {'row'}, use_global_device_ids=true, to_apply=%region_13.17 | all-reduce | flops 1024 | bytes 8192 | tf_op jit(solution)/shard_map/psum | solution.py:98
  463.2 52.4 %all-reduce.11.cloned.1.call-done = f32[8,64,64]{1,2,0:T(8,128)} async-done(((f32[8,64,64]{1,2,0:T(8,128)}), f32[8,64,64]{1,2,0:T(8,128)}) %all-reduce.11.cloned.1.call-update) | async-done | bytes 131088 | tf_op jit(solution)/shard_map/psum | solution.py:98
  518.1 11.7 %custom-call.20 = f32[2,64,64]{2,1,0:T(8,128)S(1)} custom-call(f32[2,64,64]{2,1,0:T(8,128)S(1)} %fusion.127), custom_call_target="Cholesky" | custom-call | tf_op jit(solution)/shard_map/jit(cholesky)/cholesky | solution.py:46
  530.1 9.8 %custom-call.21 = f32[2,1,64,64]{2,3,1,0:T(8,128)S(1)} custom-call(f32[2,1,64,64]{3,2,1,0:T(8,128)S(1)} %select_bitcast_fusion.4), custom_call_target="InvertDiagBlocksLowerTriangular" | custom-call | tf_op jit(solution)/shard_map/vmap(jit(_cho_solve))/triangular_solve | solution.py:49
  540.8 4.6 collective-permute-done.27
  545.4 4.6 collective-permute-done.28
  550.0 4.6 collective-permute-done.29
  554.5 4.6 collective-permute-done.30
  559.1 4.6 collective-permute-done.31
  563.7 4.6 collective-permute-done.32
  568.5 4.6 collective-permute-done.33
  585.7 4.4 collective-permute-done.35
  (229 shorter events, 103.2 us)
Async XLA Ops:
  6.5 70.1 %all-reduce.5.cloned.1.call-start = ((), (), s32[]{:S(2)}) async-start(), calls=%async_computation | async-start | bytes 524288 | tf_op jit(solution)/shard_map/psum | solution.py:98
  19.9 202.7 %all-reduce.7.cloned.1.call-start = ((), (), s32[]{:S(2)}) async-start(), calls=%async_computation.1 | async-start | bytes 524288 | tf_op jit(solution)/shard_map/psum | solution.py:98
  101.7 4.6 collective-permute-start
  106.4 4.6 collective-permute-start.1
  110.9 4.6 collective-permute-start.2
  115.5 4.6 collective-permute-start.3
  120.1 4.6 collective-permute-start.4
  124.7 4.6 collective-permute-start.5
  129.3 4.7 collective-permute-start.6
  141.8 7.9 %collective-permute-start.7 = (f32[64,1024]{1,0:T(8,128)S(1)}, f32[64,1024]{1,0:T(8,128)S(1)}, u32[]{:S(2)}, u32[]{:S(2)}) collective-permute-start(f32[64,1024]{1,0:T(8,128)S(1)} %get-tuple-element.37), channel_id=1, source_target_pairs={{0,1},{1,2},{2,3},{4,5},{5,6},{6,7},{8,9},{9,10},{10,11},{12,13},{... | collective-permute-start | bytes 786440 | tf_op jit(solution)/shard_map/ppermute | solution.py:13
  145.2 8.3 %collective-permute-start.8 = (f32[64,1024]{1,0:T(8,128)S(1)}, f32[64,1024]{1,0:T(8,128)S(1)}, u32[]{:S(2)}, u32[]{:S(2)}) collective-permute-start(f32[64,1024]{1,0:T(8,128)S(1)} %get-tuple-element.35), channel_id=1, source_target_pairs={{1,0},{2,1},{3,2},{5,4},{6,5},{7,6},{9,8},{10,9},{11,10},{13,12},{... | collective-permute-start | bytes 786440 | tf_op jit(solution)/shard_map/ppermute | solution.py:13
  170.1 199.3 %all-reduce.9.cloned.1.call-start = ((), (), s32[]{:S(2)}) async-start(), calls=%async_computation.2 | async-start | bytes 524288 | tf_op jit(solution)/shard_map/psum | solution.py:98
  225.0 60.6 %copy-start.10 = (f32[1,64,1024]{2,1,0:T(8,128)S(1)}, f32[1,64,1024]{2,1,0:T(8,128)}, u32[]{:S(2)}) copy-start(f32[1,64,1024]{2,1,0:T(8,128)} %copy-done.9) | copy-start | bytes 786436
  225.1 60.6 %copy-start.18 = (f32[1,64,1024]{2,1,0:T(8,128)S(1)}, f32[1,64,1024]{2,1,0:T(8,128)}, u32[]{:S(2)}) copy-start(f32[1,64,1024]{2,1,0:T(8,128)} %copy-done.17) | copy-start | bytes 786436
  225.1 60.6 %copy-start.20 = (f32[1,64,1024]{2,1,0:T(8,128)S(1)}, f32[1,64,1024]{2,1,0:T(8,128)}, u32[]{:S(2)}) copy-start(f32[1,64,1024]{2,1,0:T(8,128)} %copy-done.19) | copy-start | bytes 786436
  251.2 34.5 %copy-start.8 = (f32[6,64,1024]{2,1,0:T(8,128)S(1)}, f32[6,64,1024]{2,1,0:T(8,128)}, u32[]{:S(2)}) copy-start(f32[6,64,1024]{2,1,0:T(8,128)} %copy-done.7) | copy-start | bytes 4718596
  251.8 4.9 collective-permute-start.9
  256.6 4.6 collective-permute-start.10
  261.2 4.6 collective-permute-start.11
  265.8 4.6 collective-permute-start.12
  270.4 4.6 collective-permute-start.13
  275.0 4.6 collective-permute-start.14
  279.6 4.6 collective-permute-start.15
  289.6 7.3 %collective-permute-start.16 = (f32[64,1024]{1,0:T(8,128)S(1)}, f32[64,1024]{1,0:T(8,128)S(1)}, u32[]{:S(2)}, u32[]{:S(2)}) collective-permute-start(f32[64,1024]{1,0:T(8,128)S(1)} %get-tuple-element.32), channel_id=1, source_target_pairs={{0,1},{1,2},{2,3},{4,5},{5,6},{6,7},{8,9},{9,10},{10,11},{12,13},{... | collective-permute-start | bytes 786440 | tf_op jit(solution)/shard_map/ppermute | solution.py:13
  293.0 8.3 %collective-permute-start.17 = (f32[64,1024]{1,0:T(8,128)S(1)}, f32[64,1024]{1,0:T(8,128)S(1)}, u32[]{:S(2)}, u32[]{:S(2)}) collective-permute-start(f32[64,1024]{1,0:T(8,128)S(1)} %get-tuple-element.30), channel_id=1, source_target_pairs={{1,0},{2,1},{3,2},{5,4},{6,5},{7,6},{9,8},{10,9},{11,10},{13,12},{... | collective-permute-start | bytes 786440 | tf_op jit(solution)/shard_map/ppermute | solution.py:13
  316.9 198.7 %all-reduce.11.cloned.1.call-start = ((), (), s32[]{:S(2)}) async-start(), calls=%async_computation.3 | async-start | bytes 524288 | tf_op jit(solution)/shard_map/psum | solution.py:98
  371.9 60.4 %copy-start.12 = (f32[1,64,1024]{2,1,0:T(8,128)S(1)}, f32[1,64,1024]{2,1,0:T(8,128)}, u32[]{:S(2)}) copy-start(f32[1,64,1024]{2,1,0:T(8,128)} %copy-done.11) | copy-start | bytes 786436
  371.9 60.3 %copy-start.14 = (f32[1,64,1024]{2,1,0:T(8,128)S(1)}, f32[1,64,1024]{2,1,0:T(8,128)}, u32[]{:S(2)}) copy-start(f32[1,64,1024]{2,1,0:T(8,128)} %copy-done.13) | copy-start | bytes 786436
  371.9 60.3 %copy-start.16 = (f32[1,64,1024]{2,1,0:T(8,128)S(1)}, f32[1,64,1024]{2,1,0:T(8,128)}, u32[]{:S(2)}) copy-start(f32[1,64,1024]{2,1,0:T(8,128)} %copy-done.15) | copy-start | bytes 786436
  398.6 4.6 collective-permute-start.18
  403.2 4.6 collective-permute-start.19
  407.8 4.6 collective-permute-start.20
  412.4 4.6 collective-permute-start.21
  417.0 4.6 collective-permute-start.22
  421.6 4.6 collective-permute-start.23
  426.2 4.6 collective-permute-start.24
  436.2 7.3 %collective-permute-start.25 = (f32[64,1024]{1,0:T(8,128)S(1)}, f32[64,1024]{1,0:T(8,128)S(1)}, u32[]{:S(2)}, u32[]{:S(2)}) collective-permute-start(f32[64,1024]{1,0:T(8,128)S(1)} %get-tuple-element.27), channel_id=1, source_target_pairs={{0,1},{1,2},{2,3},{4,5},{5,6},{6,7},{8,9},{9,10},{10,11},{12,13},{... | collective-permute-start | bytes 786440 | tf_op jit(solution)/shard_map/ppermute | solution.py:13
  439.6 8.3 %collective-permute-start.26 = (f32[64,1024]{1,0:T(8,128)S(1)}, f32[64,1024]{1,0:T(8,128)S(1)}, u32[]{:S(2)}, u32[]{:S(2)}) collective-permute-start(f32[64,1024]{1,0:T(8,128)S(1)} %get-tuple-element.25), channel_id=1, source_target_pairs={{1,0},{2,1},{3,2},{5,4},{6,5},{7,6},{9,8},{10,9},{11,10},{13,12},{... | collective-permute-start | bytes 786440 | tf_op jit(solution)/shard_map/ppermute | solution.py:13
  540.1 34.5 %copy-start.4 = (f32[6,64,1024]{2,1,0:T(8,128)S(1)}, f32[6,64,1024]{2,1,0:T(8,128)}, u32[]{:S(2)}) copy-start(f32[6,64,1024]{2,1,0:T(8,128)} %copy-done.3) | copy-start | bytes 4718596
  540.7 4.6 collective-permute-start.27
  545.4 4.6 collective-permute-start.28
  550.0 4.6 collective-permute-start.29
  554.5 4.6 collective-permute-start.30
  559.1 4.6 collective-permute-start.31
  563.7 4.6 collective-permute-start.32
  568.3 4.8 collective-permute-start.33
  578.5 7.3 %collective-permute-start.34 = (f32[64,1024]{1,0:T(8,128)S(1)}, f32[64,1024]{1,0:T(8,128)S(1)}, u32[]{:S(2)}, u32[]{:S(2)}) collective-permute-start(f32[64,1024]{1,0:T(8,128)S(1)} %get-tuple-element.20), channel_id=1, source_target_pairs={{0,1},{1,2},{2,3},{4,5},{5,6},{6,7},{8,9},{9,10},{10,11},{12,13},{... | collective-permute-start | bytes 786440 | tf_op jit(solution)/shard_map/ppermute | solution.py:13
  581.9 8.3 %collective-permute-start.35 = (f32[64,1024]{1,0:T(8,128)S(1)}, f32[64,1024]{1,0:T(8,128)S(1)}, u32[]{:S(2)}, u32[]{:S(2)}) collective-permute-start(f32[64,1024]{1,0:T(8,128)S(1)} %get-tuple-element.21), channel_id=1, source_target_pairs={{1,0},{2,1},{3,2},{5,4},{6,5},{7,6},{9,8},{10,9},{11,10},{13,12},{... | collective-permute-start | bytes 786440 | tf_op jit(solution)/shard_map/ppermute | solution.py:13
  (13 other events, 92.6 us)
Sparse Core Ops, SparseCore 0:
  20.0 56.6 all-reduce.4
  170.2 52.3 all-reduce.6
  317.0 52.3 all-reduce.8
  463.2 52.3 all-reduce.10
